TPU v7x, 256 devices: a whole 4x4x8 slice. The times are simulated.
256 devices in a mesh: row: 8 (over z), col: 8 (over y, core), depth: 4 (over x).
Axes of the slice: x: 4, y: 4, z: 8, core: 2. Of those that a mesh axis runs over, the one named last changes fastest.
Arguments:
- a21_leaf: float32 [4, 4096, 2048], P('depth', 'row', 'col'), may hold values from -1.2 to 1.2
- a12_leaf: float32 [4, 2048, 4096], P('depth', 'row', 'col'), may hold values from -1.2 to 1.2
- uinv_leaf: float32 [4, 2048, 2048], P('depth', None, 'col'), may hold values from -0.2 to 1.5, as said below
- linv_leaf: float32 [4, 2048, 2048], P('depth', 'row'), may hold values from -0.2 to 1.5, as said below
- live: int32 [4], P('depth'), may hold values from 16 to 32
- row_map: int32 [4, 32], P('depth', 'row'), may hold values from 0 to 63, as said below
- col_map: int32 [4, 32], P('depth', 'col'), may hold values from 0 to 63, as said below
- a22_anc: float32 [8192, 8192], P(('row', 'depth'), 'col'), may hold values from -6 to 6
- a21_anc: float32 [8192, 2048], P(('row', 'depth'), 'col'), may hold values from -1.2 to 1.2
- a12_anc: float32 [2048, 8192], P(('row', 'depth'), 'col'), may hold values from -1.2 to 1.2
- uinv_anc: float32 [2048, 2048], P(None, 'col'), may hold values from -0.2 to 1.5, as said below
- linv_anc: float32 [2048, 2048], P(('row', 'depth')), may hold values from -0.2 to 1.5, as said below
Outputs:
- leaf_lower: float32 [4, 4096, 2048], P('depth', 'row', 'col')
- leaf_upper: float32 [4, 2048, 4096], P('depth', 'row', 'col')
- anc_lower: float32 [8192, 2048], P(('row', 'depth'), 'col')
- anc_upper: float32 [2048, 8192], P(('row', 'depth'), 'col')
- anc_schur: float32 [8192, 8192], P(('row', 'depth'), 'col')
Inputs may be any that keep to these rules, and one draw needn't show every extreme that they name: `uinv_leaf`: upper triangular: zero below the diagonal, diagonal between 0.5 and 1.5. `linv_leaf`: lower triangular: zero above the diagonal, diagonal between 0.5 and 1.5. `uinv_anc`: upper triangular: zero below the diagonal, diagonal between 0.5 and 1.5. `linv_anc`: lower triangular: zero above the diagonal, diagonal between 0.5 and 1.5. `row_map`: within one replica the entries are distinct. Leaf block row i lies in the k-th of 8 equal ranges of leaf block rows, and its target lies in the k-th of 8 equal ranges of the 64 ancestor block rows. `col_map`: within one replica the entries are distinct. Leaf block column j lies in the k-th of 8 equal ranges of leaf block columns, and its target lies in the k-th of 8 equal ranges of the 64 ancestor block columns.
All inputs are finite; a program needn't handle non-finite values.
Results may differ from a plain program's by a relative error of at most 0.0001.
Values sent between devices are 32-bit elements; how exact they have to be, the bound alone decides.
No kernel may reach another device: no remote copies, remote signals or barrier semaphores. Data moves between devices by JAX's collectives and lax.ppermute only.
A program may use at most 128 MiB of HBM per device.

v0:
```python
import math
import jax
import jax.numpy as jnp
from jax import lax
from jax.sharding import PartitionSpec as P

NB = 128


def in_one_piece(arrays, axis, split_dim, concat_dim, along):
    widths = [math.prod(a.shape[along:]) for a in arrays]
    both = jnp.concatenate(
        [a.reshape(*a.shape[:along], w) for a, w in zip(arrays, widths)], axis=along
    )
    out = lax.all_to_all(both, axis, split_axis=split_dim, concat_axis=concat_dim, tiled=True)
    tiles = jnp.split(out, [sum(widths[:k]) for k in range(1, len(widths))], axis=along)
    return tuple((b.reshape(*out.shape[:along], *a.shape[along:]) for a, b in zip(arrays, tiles)))


def sent_to_all(shard, axis):
    copies = jnp.broadcast_to(shard, (lax.axis_size(axis), *shard.shape))
    return lax.all_to_all(copies, axis, split_axis=0, concat_axis=0, tiled=True)


def in_order(tiles, dim):
    lengths = list(tiles.shape[1:])
    lengths[dim] *= tiles.shape[0]
    return jnp.moveaxis(tiles, 0, dim).reshape(lengths)


def collect(shard, axis, dim):
    tiles = sent_to_all(shard, axis)
    return in_order(tiles, dim)


def gather_axes(shard, axes, dim):
    out = shard
    for number in range(len(axes) - 1, -1, -1):
        out = lax.all_gather(out, axes[number], axis=dim, tiled=True)
    return out


def product(left, right):
    return jnp.dot(left, right, precision=lax.Precision.HIGHEST, preferred_element_type=jnp.float32)


def combine_depth(schur, row_map, col_map, a22_anc):
    block_size = NB
    rows_here = schur.shape[0]
    cols_here = schur.shape[1]
    leaf_rows = rows_here // block_size
    leaf_cols = cols_here // block_size
    anc_rows = a22_anc.shape[0]
    replicas = lax.axis_size("depth")
    anc_row_blocks = anc_rows * replicas // block_size
    anc_col_blocks = a22_anc.shape[1] // block_size
    row_local = row_map[0] - lax.axis_index("row") * anc_row_blocks
    col_local = col_map[0] - lax.axis_index("col") * anc_col_blocks
    owner_blocks = anc_rows // block_size
    slots = min(leaf_rows, owner_blocks)
    owner = row_local // owner_blocks
    earlier = lax.iota(jnp.int32, leaf_rows)[:, None] > lax.iota(jnp.int32, leaf_rows)[None, :]
    same = owner[:, None] == owner[None, :]
    rank = jnp.sum((earlier & same).astype(jnp.int32), axis=1)
    select = (
        (owner[:, None, None] == lax.iota(jnp.int32, replicas)[None, :, None])
        & (rank[:, None, None] == lax.iota(jnp.int32, slots)[None, None, :])
    ).astype(jnp.float32)
    leaf_blocks = schur.reshape(leaf_rows, block_size, cols_here)
    packed = jnp.einsum("iqs,ixc->qsxc", select, leaf_blocks, precision=lax.Precision.HIGHEST)
    packed = packed.reshape(replicas, slots * block_size, cols_here)
    target = (row_local - owner * owner_blocks + 1).astype(jnp.float32)
    tags = jnp.einsum("iqs,i->qs", select, target, precision=lax.Precision.HIGHEST) - 1.0
    col_tags = jnp.broadcast_to(col_local.astype(jnp.float32)[None, :], (replicas, leaf_cols))
    got_rows, got_tags, got_cols = in_one_piece((packed, tags, col_tags), "depth", 0, 0, 1)
    slot_pick = (
        got_tags[:, :, None] == lax.iota(jnp.int32, owner_blocks).astype(jnp.float32)[None, None, :]
    ).astype(jnp.float32)
    column_pick = (
        got_cols[:, :, None]
        == lax.iota(jnp.int32, anc_col_blocks).astype(jnp.float32)[None, None, :]
    ).astype(jnp.float32)
    pieces = got_rows.reshape(replicas, slots, block_size, leaf_cols, block_size)
    sectioned = jnp.einsum("psa,psxjy->paxjy", slot_pick, pieces, precision=lax.Precision.HIGHEST)
    placed = jnp.einsum("paxjy,pjb->axby", sectioned, column_pick, precision=lax.Precision.HIGHEST)
    return placed.reshape(anc_rows, anc_col_blocks * block_size)


def anc_panels(a21_anc, a12_anc, uinv_anc, linv_anc):
    factor = uinv_anc
    anc_lower = product(collect(a21_anc, "col", 1), factor)
    lower_whole = collect(anc_lower, "col", 1)
    factor = linv_anc
    anc_upper = product(factor, lax.all_gather(a12_anc, ("row", "depth"), axis=0, tiled=True))
    return (anc_lower, lower_whole, anc_upper)


def shards(
    a21_leaf,
    a12_leaf,
    uinv_leaf,
    linv_leaf,
    live,
    row_map,
    col_map,
    a22_anc,
    a21_anc,
    a12_anc,
    uinv_anc,
    linv_anc,
):
    block_size = NB
    panel_left = a21_leaf[0]
    panel_top = a12_leaf[0]
    upper_inverse = uinv_leaf[0]
    lower_inverse = linv_leaf[0]
    rows_here = panel_left.shape[0]
    cols_here = panel_top.shape[1]
    live_rows = live[0] * block_size
    row_pos = lax.axis_index("row") * rows_here + lax.iota(jnp.int32, rows_here)
    col_pos = lax.axis_index("col") * cols_here + lax.iota(jnp.int32, cols_here)
    row_keep = (row_pos < live_rows).astype(jnp.float32)
    col_keep = (col_pos < live_rows).astype(jnp.float32)
    factor = upper_inverse
    lower_part = product(lax.all_gather(panel_left, "col", axis=1, tiled=True), factor)
    leaf_lower = lower_part * row_keep[:, None]
    factor = lower_inverse
    upper_part = product(factor, lax.all_gather(panel_top, "row", axis=0, tiled=True))
    leaf_upper = upper_part * col_keep[None, :]
    upper_whole = lax.all_gather(leaf_upper, "row", axis=0, tiled=True)
    factor = upper_whole
    schur = jnp.zeros((rows_here, cols_here), jnp.float32) - product(
        lax.all_gather(leaf_lower, "col", axis=1, tiled=True), factor
    )
    own_update = combine_depth(schur, row_map, col_map, a22_anc)
    anc_lower, lower_whole, anc_upper = anc_panels(a21_anc, a12_anc, uinv_anc, linv_anc)
    factor = lower_whole
    anc_schur = a22_anc + own_update - product(factor, gather_axes(anc_upper, ("row", "depth"), 0))
    return (leaf_lower[None], leaf_upper[None], anc_lower, anc_upper, anc_schur)


def solution(mesh):
    in_specs = (
        P("depth", "row", "col"),
        P("depth", "row", "col"),
        P("depth", None, "col"),
        P("depth", "row", None),
        P("depth"),
        P("depth", "row"),
        P("depth", "col"),
        P(("row", "depth"), "col"),
        P(("row", "depth"), "col"),
        P(("row", "depth"), "col"),
        P(None, "col"),
        P(("row", "depth"), None),
    )
    out_specs = (
        P("depth", "row", "col"),
        P("depth", "row", "col"),
        P(("row", "depth"), "col"),
        P(("row", "depth"), "col"),
        P(("row", "depth"), "col"),
    )
    return jax.shard_map(shards, mesh=mesh, in_specs=in_specs, out_specs=out_specs, check_vma=False)
```

profile of v0, /device:TPU:1, one launch (start us, length us, event | category | flops | bytes accessed | tf_op | source)
XLA Modules:
  0.0 436.7 jit_solution(4254180319421357973)
XLA Ops:
  7.2 0.0 copy-start
  7.2 0.0 all-gather.20.cloned.1.call-start
  7.2 0.7 all-gather.20.cloned.1.call-update
  7.9 0.0 all-gather.22.cloned.1.call-start
  8.0 0.7 all-gather.22.cloned.1.call-update
  8.7 0.0 all-gather.10.cloned.1.call-start
  8.7 0.7 all-gather.10.cloned.1.call-update
  9.4 0.0 all-gather.12.cloned.1.call-start
  10.1 38.6 %all-gather.20.cloned.1.call-done = f32[1,512,2048]{2,1,0:T(8,128)} async-done(((f32[1,512,256]{2,1,0:T(8,128)}), f32[1,512,2048]{2,1,0:T(8,128)}) %all-gather.20.cloned.1.call-update) | async-done | bytes 4194320 | tf_op jit(solution)/shard_map/all_gather | solution.py:125
  48.7 0.0 copy-done
  48.7 6.4 %fusion.10 = f32[512,256]{1,0:T(8,128)} fusion(f32[1,2048,256]{2,1,0:T(8,128)S(1)} %copy-done, f32[1,512,2048]{2,1,0:T(8,128)} %all-gather.20.cloned.1.call-done, f32[512]{0:T(512)S(1)} %fusion.32), kind=kOutput, calls=%fused_computation.13 | convolution fusion | flops 3221356544 | bytes 6817792 | tf_op jit(solution)/shard_map/dot_general | solution.py:44
  55.1 0.0 all-gather.12.cloned.1.call-update
  55.1 0.0 all-gather.14.cloned.1.call-start
  55.2 0.0 copy-start.4
  55.2 49.4 %all-gather.22.cloned.1.call-done = f32[1,2048,512]{2,1,0:T(8,128)} async-done(((f32[1,256,512]{2,1,0:T(8,128)}), f32[1,2048,512]{2,1,0:T(8,128)}) %all-gather.22.cloned.1.call-update) | async-done | bytes 4194320 | tf_op jit(solution)/shard_map/all_gather | solution.py:128
  104.6 7.3 %fusion.15 = f32[256,512]{1,0:T(8,128)} fusion(f32[1,2048,512]{2,1,0:T(8,128)} %all-gather.22.cloned.1.call-done, f32[1,256,2048]{2,1,0:T(8,128)} %param.15, f32[512]{0:T(512)S(1)} %fusion.33), kind=kOutput, calls=%fused_computation.14 | convolution fusion | flops 3221356544 | bytes 6817792 | tf_op jit(solution)/shard_map/dot_general | solution.py:44
  111.9 0.0 all-gather.14.cloned.1.call-update
  112.0 0.0 copy-done.4
  112.0 0.1 copy.29
  112.1 1.5 broadcast_in_dim.16
  113.6 0.0 copy-start.5
  113.6 5.3 %all-to-all-start = ((f32[8,256,256]{1,2,0:T(8,128)}), f32[8,256,256]{1,2,0:T(8,128)S(1)}, u32[]{:S(2)}, u32[]{:S(2)}) async-start(f32[8,256,256]{1,2,0:T(8,128)} %broadcast_in_dim.16), calls=%async_computation | async-start | bytes 4194304 | tf_op jit(solution)/shard_map/all_to_all | solution.py:22
  118.9 0.0 all-gather.16.cloned.1.call-start
  118.9 0.0 copy-done.5
  118.9 0.1 convert_reduce_fusion
  119.0 84.1 %all-gather.10.cloned.1.call-done = f32[2048,1024]{1,0:T(8,128)} async-done(((f32[64,1024]{1,0:T(8,128)}), f32[2048,1024]{1,0:T(8,128)}) %all-gather.10.cloned.1.call-update) | async-done | bytes 8388624 | tf_op jit(solution)/shard_map/all_gather | solution.py:94
  203.1 0.0 copy-done.3
  203.1 8.2 %fusion.51 = f32[64,1024]{1,0:T(8,128)} fusion(f32[64,2048]{1,0:T(8,128)S(1)} %copy-done.3, f32[2048,1024]{1,0:T(8,128)} %all-gather.10.cloned.1.call-done), kind=kOutput, calls=%fused_computation.69 | convolution fusion | flops 1610612736 | bytes 9175040 | tf_op jit(solution)/shard_map/dot_general | solution.py:44
  211.3 0.0 all-gather.16.cloned.1.call-update
  211.4 0.2 all-gather.18.cloned.1.call-start
  211.6 0.1 fusion.27
  211.7 0.1 copy.37
  211.8 0.0 copy-done.6
  211.8 0.1 bitcast_add_fusion.1
  211.9 26.4 %all-gather.12.cloned.1.call-done = f32[512,2048]{1,0:T(8,128)} async-done(((f32[512,256]{1,0:T(8,128)}), f32[512,2048]{1,0:T(8,128)}) %all-gather.12.cloned.1.call-update) | async-done | bytes 4194320 | tf_op jit(solution)/shard_map/all_gather | solution.py:133
  238.3 56.4 %all-gather.14.cloned.1.call-done = f32[2048,512]{1,0:T(8,128)} async-done(((f32[256,512]{1,0:T(8,128)}), f32[2048,512]{1,0:T(8,128)}) %all-gather.14.cloned.1.call-update) | async-done | bytes 4194320 | tf_op jit(solution)/shard_map/all_gather | solution.py:130
  294.7 9.4 %convolution_subtract_fusion = f32[512,512]{1,0:T(8,128)S(1)} fusion(f32[512,2048]{1,0:T(8,128)} %all-gather.12.cloned.1.call-done, f32[2048,512]{1,0:T(8,128)} %all-gather.14.cloned.1.call-done), kind=kOutput, calls=%fused_computation.11 | convolution fusion | flops 6442713088 | bytes 9437184 | tf_op jit(solution)/shard_map/dot_general | solution.py:44
  304.0 3.6 fusion.20
  307.6 12.7 %all-gather.16.cloned.1.call-done = f32[256,1024]{1,0:T(8,128)} async-done(((f32[64,1024]{1,0:T(8,128)}), f32[256,1024]{1,0:T(8,128)}) %all-gather.16.cloned.1.call-update) | async-done | bytes 1048592 | tf_op jit(solution)/shard_map/all_gather | solution.py:39
  320.3 0.0 all-gather.18.cloned.1.call-update
  320.3 3.1 constant_dynamic-update-slice_fusion
  323.4 1.3 dynamic-update-slice.1
  324.7 1.4 dynamic-update-slice.2
  326.0 4.8 %copy.31 = f32[4,1,131078]{2,1,0:T(1,128)} copy(f32[4,1,131078]{2,0,1:T(4,128)} %bitcast.99) | data formatting | bytes 4194496 | tf_op jit(solution)/shard_map/all_to_all | solution.py:15
  330.9 0.0 all-to-all-done
  330.9 4.5 %all-to-all-start.1 = ((f32[4,1,131078]{2,1,0:T(1,128)}), f32[4,1,131078]{2,1,0:T(1,128)}, u32[]{:S(2)}, u32[]{:S(2)}) async-start(f32[4,1,131078]{2,1,0:T(1,128)} %copy.31), calls=%async_computation.1 | async-start | bytes 4198400 | tf_op jit(solution)/shard_map/all_to_all | solution.py:15
  335.4 5.3 %fusion.50 = f32[256,256]{1,0:T(8,128)S(1)} fusion(f32[256,2048]{0,1:T(8,128)S(1)} %bitcast.100, f32[2048,256]{1,0:T(8,128)} %param.22), kind=kOutput, calls=%fused_computation.68 | convolution fusion | flops 1610612736 | bytes 4456448 | tf_op jit(solution)/shard_map/dot_general | solution.py:44
  340.7 0.0 copy-start.2
  340.7 0.1 copy.35
  340.8 18.3 %all-to-all-done.1 = f32[4,1,131078]{2,1,0:T(1,128)} async-done(((f32[4,1,131078]{2,1,0:T(1,128)}), f32[4,1,131078]{2,1,0:T(1,128)}, u32[]{:S(2)}, u32[]{:S(2)}) %all-to-all-start.1) | async-done | bytes 2097280 | tf_op jit(solution)/shard_map/all_to_all | solution.py:15
  359.1 1.5 broadcast_in_dim.20
  360.6 0.0 copy-done.2
  360.6 7.9 %all-to-all-start.2 = ((f32[8,256,256]{1,2,0:T(8,128)}), f32[8,256,256]{1,2,0:T(8,128)}, u32[]{:S(2)}, u32[]{:S(2)}) async-start(f32[8,256,256]{1,2,0:T(8,128)} %broadcast_in_dim.20), calls=%async_computation.2 | async-start | bytes 4194304 | tf_op jit(solution)/shard_map/all_to_all | solution.py:22
  368.5 2.6 copy.53
  371.2 1.5 split.14
  372.7 0.1 split.12
  372.8 3.4 reshape_reshape.7
  376.2 0.1 copy.32
  376.2 4.8 %fusion.8 = f32[4,2,128,4,128]{4,1,3,2,0:T(2,128)S(1)} fusion(f32[4,2,128,4,128]{4,3,2,1,0:T(4,128)S(1)} %reshape_reshape.7, f32[4,2]{1,0:T(4,128)S(1)} %split.13, f32[2]{0:T(128)S(1)} %iota_convert_fusion), kind=kOutput, calls=%fused_computation.9 | convolution fusion | flops 12582928 | bytes 4194344 | tf_op jit(solution)/shard_map/psa,psxjy->paxjy/dot_general | solution.py:84
  381.0 3.2 fusion.6
  384.3 10.6 %all-to-all-done.2 = f32[8,256,256]{1,2,0:T(8,128)} async-done(((f32[8,256,256]{1,2,0:T(8,128)}), f32[8,256,256]{1,2,0:T(8,128)}, u32[]{:S(2)}, u32[]{:S(2)}) %all-to-all-start.2) | async-done | bytes 2097184 | tf_op jit(solution)/shard_map/all_to_all | solution.py:22
  394.8 23.6 %all-gather.18.cloned.1.call-done = f32[2048,1024]{1,0:T(8,128)} async-done(((f32[256,1024]{1,0:T(8,128)}), f32[2048,1024]{1,0:T(8,128)}) %all-gather.18.cloned.1.call-update) | async-done | bytes 8388624 | tf_op jit(solution)/shard_map/all_gather | solution.py:39
  418.5 11.4 %convolution_subtract_fusion.1 = f32[256,1024]{1,0:T(8,128)} fusion(f32[256,2048]{0,1:T(8,128)} %bitcast.28, f32[2048,1024]{1,0:T(8,128)} %all-gather.18.cloned.1.call-done, f32[256,1024]{1,0:T(8,128)} %param.19, f32[32,8,8,128]{3,2,1,0:T(8,128)S(1)} %bitcast.103), kind=kOutput, calls=%fused_computation.12 | convolution fusion | flops 6442975232 | bytes 13631488 | tf_op jit(solution)/shard_map/dot_general | solution.py:44
  429.9 0.0 copy-done.1
  (14 shorter events, 0.1 us)
Async XLA Ops:
  7.2 41.5 %copy-start = (f32[1,2048,256]{2,1,0:T(8,128)S(1)}, f32[1,2048,256]{2,1,0:T(8,128)}, u32[]{:S(2)}) copy-start(f32[1,2048,256]{2,1,0:T(8,128)} %param.14) | copy-start | bytes 6291460
  7.2 41.5 %all-gather.20.cloned.1.call-start = ((), (), s32[]{:S(2)}) async-start(), calls=%async_computation.8 | async-start | bytes 4718592 | tf_op jit(solution)/shard_map/all_gather | solution.py:125
  7.9 96.7 %all-gather.22.cloned.1.call-start = ((), (), s32[]{:S(2)}) async-start(), calls=%async_computation.9 | async-start | bytes 4718592 | tf_op jit(solution)/shard_map/all_gather | solution.py:128
  8.7 194.5 %all-gather.10.cloned.1.call-start = ((), (), s32[]{:S(2)}) async-start(), calls=%async_computation.3 | async-start | bytes 8650752 | tf_op jit(solution)/shard_map/all_gather | solution.py:94
  9.4 228.9 %all-gather.12.cloned.1.call-start = ((), (), s32[]{:S(2)}) async-start(), calls=%async_computation.4 | async-start | bytes 4718592 | tf_op jit(solution)/shard_map/all_gather | solution.py:133
  55.1 239.5 %all-gather.14.cloned.1.call-start = ((), (), s32[]{:S(2)}) async-start(), calls=%async_computation.5 | async-start | bytes 4718592 | tf_op jit(solution)/shard_map/all_gather | solution.py:130
  55.2 56.8 %copy-start.4 = (f32[256,256]{1,0:T(8,128)S(1)}, f32[256,256]{1,0:T(8,128)}, u32[]{:S(2)}) copy-start(f32[256,256]{1,0:T(8,128)} %param.20) | copy-start | bytes 786436
  113.6 5.3 %copy-start.5 = (s32[1,4]{1,0:T(1,128)S(1)}, s32[1,4]{1,0:T(1,128)}, u32[]{:S(2)}) copy-start(s32[1,4]{1,0:T(1,128)} %param.17) | copy-start | bytes 52
  113.6 89.5 %copy-start.3 = (f32[64,2048]{1,0:T(8,128)S(1)}, f32[64,2048]{1,0:T(8,128)}, u32[]{:S(2)}) copy-start(f32[64,2048]{1,0:T(8,128)} %param.23) | copy-start | bytes 1572868
  113.6 217.2 %all-to-all-start = ((f32[8,256,256]{1,2,0:T(8,128)}), f32[8,256,256]{1,2,0:T(8,128)S(1)}, u32[]{:S(2)}, u32[]{:S(2)}) async-start(f32[8,256,256]{1,2,0:T(8,128)} %broadcast_in_dim.16), calls=%async_computation | async-start | bytes 4194304 | tf_op jit(solution)/shard_map/all_to_all | solution.py:22
  118.9 201.4 %all-gather.16.cloned.1.call-start = ((), (), s32[]{:S(2)}) async-start(), calls=%async_computation.6 | async-start | bytes 1310720 | tf_op jit(solution)/shard_map/all_gather | solution.py:39
  119.0 92.8 %copy-start.6 = (s32[1,4]{1,0:T(1,128)S(1)}, s32[1,4]{1,0:T(1,128)}, u32[]{:S(2)}) copy-start(s32[1,4]{1,0:T(1,128)} %param.18) | copy-start | bytes 52
  211.4 207.1 %all-gather.18.cloned.1.call-start = ((), (), s32[]{:S(2)}) async-start(), calls=%async_computation.7 | async-start | bytes 9437184 | tf_op jit(solution)/shard_map/all_gather | solution.py:39
  330.9 28.3 %all-to-all-start.1 = ((f32[4,1,131078]{2,1,0:T(1,128)}), f32[4,1,131078]{2,1,0:T(1,128)}, u32[]{:S(2)}, u32[]{:S(2)}) async-start(f32[4,1,131078]{2,1,0:T(1,128)} %copy.31), calls=%async_computation.1 | async-start | bytes 4198400 | tf_op jit(solution)/shard_map/all_to_all | solution.py:15
  340.7 20.0 %copy-start.2 = (f32[256,256]{1,0:T(8,128)}, f32[256,256]{1,0:T(8,128)S(1)}, u32[]{:S(2)}) copy-start(f32[256,256]{1,0:T(8,128)S(1)} %fusion.50) | copy-start | bytes 786436
  360.6 34.2 %all-to-all-start.2 = ((f32[8,256,256]{1,2,0:T(8,128)}), f32[8,256,256]{1,2,0:T(8,128)}, u32[]{:S(2)}, u32[]{:S(2)}) async-start(f32[8,256,256]{1,2,0:T(8,128)} %broadcast_in_dim.20), calls=%async_computation.2 | async-start | bytes 4194304 | tf_op jit(solution)/shard_map/all_to_all | solution.py:22
  418.5 11.4 %copy-start.1 = (f32[1,2048,256]{2,1,0:T(8,128)S(1)}, f32[1,2048,256]{2,1,0:T(8,128)}, u32[]{:S(2)}) copy-start(f32[1,2048,256]{2,1,0:T(8,128)} %param.14) | copy-start | bytes 6291460
Sparse Core Ops, SparseCore 0:
  9.8 38.8 all-gather.19
  50.5 54.1 all-gather.21
  107.2 95.8 all-gather.9
  205.4 32.8 all-gather.11
  240.5 54.1 all-gather.13
  296.9 23.3 all-gather.15
  322.0 96.3 all-gather.17
where the time goes:
time: 437 us
  waiting for transfers between devices  322 us (74%)
  matrix products  59.7 us (14%)
  local copies, waits for them, and re-layouts  21.7 us (5%)
  starting transfers between devices  18.1 us (4%)
  between operations  14.9 us (3%)
    all_gather x1, waiting for transfers between devices, anc_panels(): lax.all_gather(a12_anc, ('row', 'depth'), axis=0, tiled=True)  84.1 us
    all_gather x1, waiting for transfers between devices, shards(): upper_whole = lax.all_gather(leaf_upper, 'row', axis=0, tiled=True)  56.4 us
    all_gather x1, waiting for transfers between devices, shards(): lax.all_gather(panel_top, 'row', axis=0, tiled=True)  49.4 us
    dot_general x6, matrix products, product(): jnp.dot(left, right, precision=lax.Precision.HIGHEST, preferred_element_t...  48 us
    all_gather x1, waiting for transfers between devices, shards(): lax.all_gather(panel_left, 'col', axis=1, tiled=True)  38.6 us
    all_gather x2, waiting for transfers between devices, gather_axes(): out = lax.all_gather(out, axes[number], axis=dim, tiled=True)  36.3 us
    all_gather x1, waiting for transfers between devices, shards(): lax.all_gather(leaf_lower, 'col', axis=1, tiled=True)  26.4 us
    all_to_all x1, waiting for transfers between devices, in_one_piece(): lax.all_to_all(both, axis, split_axis=split_dim, concat_axis=concat_dim,...  18.3 us
  transfers between devices with their start and end apart: 10, of which 9 were waited for; matrix products, arithmetic and copies ran while one was open for 16% of the time, Pallas kernels for 0%

commit v1 on v0

--- a/solution.py
+++ b/solution.py
@@ -127,7 +127,10 @@
     factor = lower_inverse
     upper_part = product(factor, lax.all_gather(panel_top, "row", axis=0, tiled=True))
     leaf_upper = upper_part * col_keep[None, :]
-    upper_whole = lax.all_gather(leaf_upper, "row", axis=0, tiled=True)
+    size = lax.axis_size("row")
+    parts = jnp.stack([leaf_upper for _ in range(size)])
+    parts = lax.all_to_all(parts, "row", split_axis=0, concat_axis=0)
+    upper_whole = jnp.concatenate(parts, axis=0)
     factor = upper_whole
     schur = jnp.zeros((rows_here, cols_here), jnp.float32) - product(
         lax.all_gather(leaf_lower, "col", axis=1, tiled=True), factor

time: 437 us -> 459 us (1.050)
  waiting for transfers between devices: 322 us -> 338 us
    all_gather x1, waiting for transfers between devices: 84.1 us -> 144 us  [anc_panels(): lax.all_gather(a12_anc, ('row', 'depth'), axis=0, tiled=True)]
    all_gather x1 -> x0, waiting for transfers between devices: 56.4 us -> none  [shards(): upper_whole = lax.all_gather(leaf_upper, 'row', axis=0, tiled=True)]
    all_gather x1, waiting for transfers between devices: 26.4 us -> 38.4 us  [shards(): lax.all_gather(leaf_lower, 'col', axis=1, tiled=True)]
    all_to_all x0 -> x1, starting transfers between devices: none -> 4.73 us  [shards(): parts = lax.all_to_all(parts, 'row', split_axis=0, concat_axis=0)]
  transfers between devices with their start and end apart: 10 -> 10, of which waited for: 9 -> 8; matrix products, arithmetic and copies ran while one was open for 16% -> 16% of each run, Pallas kernels for 0% -> 0%
where the time goes in v1:
time: 459 us
  waiting for transfers between devices  338 us (74%)
  matrix products  58.6 us (13%)
  local copies, waits for them, and re-layouts  24.3 us (5%)
  starting transfers between devices  22.2 us (5%)
  between operations  15 us (3%)
    all_gather x1, waiting for transfers between devices, anc_panels(): lax.all_gather(a12_anc, ('row', 'depth'), axis=0, tiled=True)  144 us
    all_gather x1, waiting for transfers between devices, shards(): lax.all_gather(panel_top, 'row', axis=0, tiled=True)  49.5 us
    dot_general x6, matrix products, product(): jnp.dot(left, right, precision=lax.Precision.HIGHEST, preferred_element_t...  46.9 us
    all_gather x1, waiting for transfers between devices, shards(): lax.all_gather(panel_left, 'col', axis=1, tiled=True)  38.6 us
    all_gather x1, waiting for transfers between devices, shards(): lax.all_gather(leaf_lower, 'col', axis=1, tiled=True)  38.4 us
    all_gather x2, waiting for transfers between devices, gather_axes(): out = lax.all_gather(out, axes[number], axis=dim, tiled=True)  37.4 us
    all_to_all x1, waiting for transfers between devices, in_one_piece(): lax.all_to_all(both, axis, split_axis=split_dim, concat_axis=concat_dim,...  18.3 us
    all_to_all x2, starting transfers between devices, sent_to_all(): return lax.all_to_all(copies, axis, split_axis=0, concat_axis=0, tiled=True)  12.7 us
  transfers between devices with their start and end apart: 10, of which 8 were waited for; matrix products, arithmetic and copies ran while one was open for 16% of the time, Pallas kernels for 0%

profile of v1, /device:TPU:1, one launch (start us, length us, event | category | flops | bytes accessed | tf_op | source)
XLA Modules:
  0.0 458.5 jit_solution(12591166249709123237)
XLA Ops:
  7.2 0.0 copy-start
  7.2 0.0 all-gather.17.cloned.1.call-start
  7.2 0.7 all-gather.17.cloned.1.call-update
  7.9 0.0 all-gather.19.cloned.1.call-start
  8.0 0.7 all-gather.19.cloned.1.call-update
  8.7 0.0 all-gather.9.cloned.1.call-start
  8.7 0.7 all-gather.9.cloned.1.call-update
  9.4 0.0 all-gather.11.cloned.1.call-start
  10.1 38.6 %all-gather.17.cloned.1.call-done = f32[1,512,2048]{2,1,0:T(8,128)} async-done(((f32[1,512,256]{2,1,0:T(8,128)}), f32[1,512,2048]{2,1,0:T(8,128)}) %all-gather.17.cloned.1.call-update) | async-done | bytes 4194320 | tf_op jit(solution)/shard_map/all_gather | solution.py:125
  48.7 0.0 copy-done
  48.7 6.4 %fusion.10 = f32[512,256]{1,0:T(8,128)} fusion(f32[1,2048,256]{2,1,0:T(8,128)S(1)} %copy-done, f32[1,512,2048]{2,1,0:T(8,128)} %all-gather.17.cloned.1.call-done, f32[512]{0:T(512)S(1)} %fusion.32), kind=kOutput, calls=%fused_computation.13 | convolution fusion | flops 3221356544 | bytes 6817792 | tf_op jit(solution)/shard_map/dot_general | solution.py:44
  55.1 0.0 all-gather.11.cloned.1.call-update
  55.2 49.5 %all-gather.19.cloned.1.call-done = f32[1,2048,512]{2,1,0:T(8,128)} async-done(((f32[1,256,512]{2,1,0:T(8,128)}), f32[1,2048,512]{2,1,0:T(8,128)}) %all-gather.19.cloned.1.call-update) | async-done | bytes 4194320 | tf_op jit(solution)/shard_map/all_gather | solution.py:128
  104.6 6.2 %fusion.15 = f32[256,512]{1,0:T(8,128)S(1)} fusion(f32[1,2048,512]{2,1,0:T(8,128)} %all-gather.19.cloned.1.call-done, f32[1,256,2048]{2,1,0:T(8,128)} %param.15, f32[512]{0:T(512)S(1)} %fusion.33), kind=kOutput, calls=%fused_computation.14 | convolution fusion | flops 3221356544 | bytes 6817792 | tf_op jit(solution)/shard_map/dot_general | solution.py:44
  110.9 0.0 copy-start.2
  110.9 2.5 stack.2
  113.4 0.0 copy-done.2
  113.4 4.7 %all-to-all-start.1 = ((f32[8,256,512]{2,1,0:T(8,128)}), f32[8,256,512]{2,1,0:T(8,128)}, u32[]{:S(2)}, u32[]{:S(2)}) async-start(f32[8,256,512]{2,1,0:T(8,128)} %stack.2), calls=%async_computation.1 | async-start | bytes 8388608 | tf_op jit(solution)/shard_map/all_to_all | solution.py:132
  118.1 0.0 all-gather.13.cloned.1.call-start
  118.2 0.0 copy-done.6
  118.2 0.1 convert_reduce_fusion
  118.3 0.0 copy-start.7
  118.3 143.5 %all-gather.9.cloned.1.call-done = f32[2048,1024]{1,0:T(8,128)} async-done(((f32[64,1024]{1,0:T(8,128)}), f32[2048,1024]{1,0:T(8,128)}) %all-gather.9.cloned.1.call-update) | async-done | bytes 8388624 | tf_op jit(solution)/shard_map/all_gather | solution.py:94
  261.8 0.0 copy-done.4
  261.8 8.2 %fusion.51 = f32[64,1024]{1,0:T(8,128)} fusion(f32[64,2048]{1,0:T(8,128)S(1)} %copy-done.4, f32[2048,1024]{1,0:T(8,128)} %all-gather.9.cloned.1.call-done), kind=kOutput, calls=%fused_computation.69 | convolution fusion | flops 1610612736 | bytes 9175040 | tf_op jit(solution)/shard_map/dot_general | solution.py:44
  270.0 0.0 all-gather.13.cloned.1.call-update
  270.1 0.1 fusion.27
  270.2 0.1 copy.37
  270.3 0.0 copy-done.5
  270.3 0.2 copy.29
  270.5 0.0 copy-done.7
  270.5 0.0 all-to-all-done.1
  270.5 1.5 broadcast_in_dim.16
  272.1 4.8 %all-to-all-start = ((f32[8,256,256]{1,2,0:T(8,128)}), f32[8,256,256]{1,2,0:T(8,128)S(1)}, u32[]{:S(2)}, u32[]{:S(2)}) async-start(f32[8,256,256]{1,2,0:T(8,128)} %broadcast_in_dim.16), calls=%async_computation | async-start | bytes 4194304 | tf_op jit(solution)/shard_map/all_to_all | solution.py:22
  276.9 0.0 all-gather.15.cloned.1.call-start
  276.9 38.4 %all-gather.11.cloned.1.call-done = f32[512,2048]{1,0:T(8,128)} async-done(((f32[512,256]{1,0:T(8,128)}), f32[512,2048]{1,0:T(8,128)}) %all-gather.11.cloned.1.call-update) | async-done | bytes 4194320 | tf_op jit(solution)/shard_map/all_gather | solution.py:136
  315.3 9.4 %convolution_subtract_fusion = f32[512,512]{1,0:T(8,128)S(1)} fusion(f32[512,2048]{1,0:T(8,128)} %all-gather.11.cloned.1.call-done, f32[2048,512]{1,0:T(8,128)} %bitcast.13), kind=kOutput, calls=%fused_computation.11 | convolution fusion | flops 6442713088 | bytes 9437184 | tf_op jit(solution)/shard_map/dot_general | solution.py:44
  324.7 3.6 fusion.20
  328.2 13.9 %all-gather.13.cloned.1.call-done = f32[256,1024]{1,0:T(8,128)} async-done(((f32[64,1024]{1,0:T(8,128)}), f32[256,1024]{1,0:T(8,128)}) %all-gather.13.cloned.1.call-update) | async-done | bytes 1048592 | tf_op jit(solution)/shard_map/all_gather | solution.py:39
  342.2 0.0 all-gather.15.cloned.1.call-update
  342.2 3.1 constant_dynamic-update-slice_fusion
  345.3 1.3 dynamic-update-slice.1
  346.6 1.4 dynamic-update-slice.2
  347.9 4.8 %copy.31 = f32[4,1,131078]{2,1,0:T(1,128)} copy(f32[4,1,131078]{2,0,1:T(4,128)} %bitcast.100) | data formatting | bytes 4194496 | tf_op jit(solution)/shard_map/all_to_all | solution.py:15
  352.8 0.0 all-to-all-done
  352.8 4.5 all-to-all-start.2
  357.3 5.3 %fusion.50 = f32[256,256]{1,0:T(8,128)S(1)} fusion(f32[256,2048]{0,1:T(8,128)S(1)} %bitcast.101, f32[2048,256]{1,0:T(8,128)} %param.22), kind=kOutput, calls=%fused_computation.68 | convolution fusion | flops 1610612736 | bytes 4456448 | tf_op jit(solution)/shard_map/dot_general | solution.py:44
  362.6 0.0 copy-start.3
  362.6 0.1 copy.35
  362.7 18.3 %all-to-all-done.2 = f32[4,1,131078]{2,1,0:T(1,128)} async-done(((f32[4,1,131078]{2,1,0:T(1,128)}), f32[4,1,131078]{2,1,0:T(1,128)}, u32[]{:S(2)}, u32[]{:S(2)}) %all-to-all-start.2) | async-done | bytes 2097280 | tf_op jit(solution)/shard_map/all_to_all | solution.py:15
  381.1 1.5 broadcast_in_dim.20
  382.6 0.0 copy-done.3
  382.6 7.9 %all-to-all-start.3 = ((f32[8,256,256]{1,2,0:T(8,128)}), f32[8,256,256]{1,2,0:T(8,128)}, u32[]{:S(2)}, u32[]{:S(2)}) async-start(f32[8,256,256]{1,2,0:T(8,128)} %broadcast_in_dim.20), calls=%async_computation.3 | async-start | bytes 4194304 | tf_op jit(solution)/shard_map/all_to_all | solution.py:22
  390.5 2.6 copy.53
  393.1 1.5 split.14
  394.6 0.1 split.12
  394.7 3.4 reshape_reshape.7
  398.1 0.1 copy.32
  398.2 4.8 %fusion.8 = f32[4,2,128,4,128]{4,1,3,2,0:T(2,128)S(1)} fusion(f32[4,2,128,4,128]{4,3,2,1,0:T(4,128)S(1)} %reshape_reshape.7, f32[4,2]{1,0:T(4,128)S(1)} %split.13, f32[2]{0:T(128)S(1)} %iota_convert_fusion), kind=kOutput, calls=%fused_computation.9 | convolution fusion | flops 12582928 | bytes 4194344 | tf_op jit(solution)/shard_map/psa,psxjy->paxjy/dot_general | solution.py:84
  403.0 3.2 fusion.6
  406.2 10.6 %all-to-all-done.3 = f32[8,256,256]{1,2,0:T(8,128)} async-done(((f32[8,256,256]{1,2,0:T(8,128)}), f32[8,256,256]{1,2,0:T(8,128)}, u32[]{:S(2)}, u32[]{:S(2)}) %all-to-all-start.3) | async-done | bytes 2097184 | tf_op jit(solution)/shard_map/all_to_all | solution.py:22
  416.8 23.5 %all-gather.15.cloned.1.call-done = f32[2048,1024]{1,0:T(8,128)} async-done(((f32[256,1024]{1,0:T(8,128)}), f32[2048,1024]{1,0:T(8,128)}) %all-gather.15.cloned.1.call-update) | async-done | bytes 8388624 | tf_op jit(solution)/shard_map/all_gather | solution.py:39
  440.2 11.4 %convolution_subtract_fusion.1 = f32[256,1024]{1,0:T(8,128)} fusion(f32[256,2048]{0,1:T(8,128)} %bitcast.29, f32[2048,1024]{1,0:T(8,128)} %all-gather.15.cloned.1.call-done, f32[256,1024]{1,0:T(8,128)} %param.19, f32[32,8,8,128]{3,2,1,0:T(8,128)S(1)} %bitcast.104), kind=kOutput, calls=%fused_computation.12 | convolution fusion | flops 6442975232 | bytes 13631488 | tf_op jit(solution)/shard_map/dot_general | solution.py:44
  451.7 0.0 copy-done.1
  (16 shorter events, 0.1 us)
Async XLA Ops:
  7.2 41.5 %copy-start = (f32[1,2048,256]{2,1,0:T(8,128)S(1)}, f32[1,2048,256]{2,1,0:T(8,128)}, u32[]{:S(2)}) copy-start(f32[1,2048,256]{2,1,0:T(8,128)} %param.14) | copy-start | bytes 6291460
  7.2 41.5 %all-gather.17.cloned.1.call-start = ((), (), s32[]{:S(2)}) async-start(), calls=%async_computation.8 | async-start | bytes 4718592 | tf_op jit(solution)/shard_map/all_gather | solution.py:125
  7.9 96.7 %all-gather.19.cloned.1.call-start = ((), (), s32[]{:S(2)}) async-start(), calls=%async_computation.9 | async-start | bytes 4718592 | tf_op jit(solution)/shard_map/all_gather | solution.py:128
  8.7 253.2 %all-gather.9.cloned.1.call-start = ((), (), s32[]{:S(2)}) async-start(), calls=%async_computation.4 | async-start | bytes 8650752 | tf_op jit(solution)/shard_map/all_gather | solution.py:94
  9.4 305.9 %all-gather.11.cloned.1.call-start = ((), (), s32[]{:S(2)}) async-start(), calls=%async_computation.5 | async-start | bytes 4718592 | tf_op jit(solution)/shard_map/all_gather | solution.py:136
  110.9 2.5 copy-start.2
  113.4 4.8 %copy-start.6 = (s32[1,4]{1,0:T(1,128)S(1)}, s32[1,4]{1,0:T(1,128)}, u32[]{:S(2)}) copy-start(s32[1,4]{1,0:T(1,128)} %param.17) | copy-start | bytes 52
  113.4 148.5 %copy-start.4 = (f32[64,2048]{1,0:T(8,128)S(1)}, f32[64,2048]{1,0:T(8,128)}, u32[]{:S(2)}) copy-start(f32[64,2048]{1,0:T(8,128)} %param.23) | copy-start | bytes 1572868
  113.4 157.2 %all-to-all-start.1 = ((f32[8,256,512]{2,1,0:T(8,128)}), f32[8,256,512]{2,1,0:T(8,128)}, u32[]{:S(2)}, u32[]{:S(2)}) async-start(f32[8,256,512]{2,1,0:T(8,128)} %stack.2), calls=%async_computation.1 | async-start | bytes 8388608 | tf_op jit(solution)/shard_map/all_to_all | solution.py:132
  118.1 224.1 %all-gather.13.cloned.1.call-start = ((), (), s32[]{:S(2)}) async-start(), calls=%async_computation.6 | async-start | bytes 1310720 | tf_op jit(solution)/shard_map/all_gather | solution.py:39
  118.3 152.0 %copy-start.5 = (f32[256,256]{1,0:T(8,128)S(1)}, f32[256,256]{1,0:T(8,128)}, u32[]{:S(2)}) copy-start(f32[256,256]{1,0:T(8,128)} %param.20) | copy-start | bytes 786436
  118.3 152.2 %copy-start.7 = (s32[1,4]{1,0:T(1,128)S(1)}, s32[1,4]{1,0:T(1,128)}, u32[]{:S(2)}) copy-start(s32[1,4]{1,0:T(1,128)} %param.18) | copy-start | bytes 52
  272.1 80.7 %all-to-all-start = ((f32[8,256,256]{1,2,0:T(8,128)}), f32[8,256,256]{1,2,0:T(8,128)S(1)}, u32[]{:S(2)}, u32[]{:S(2)}) async-start(f32[8,256,256]{1,2,0:T(8,128)} %broadcast_in_dim.16), calls=%async_computation | async-start | bytes 4194304 | tf_op jit(solution)/shard_map/all_to_all | solution.py:22
  276.9 163.3 %all-gather.15.cloned.1.call-start = ((), (), s32[]{:S(2)}) async-start(), calls=%async_computation.7 | async-start | bytes 9437184 | tf_op jit(solution)/shard_map/all_gather | solution.py:39
  352.8 28.3 %all-to-all-start.2 = ((f32[4,1,131078]{2,1,0:T(1,128)}), f32[4,1,131078]{2,1,0:T(1,128)}, u32[]{:S(2)}, u32[]{:S(2)}) async-start(f32[4,1,131078]{2,1,0:T(1,128)} %copy.31), calls=%async_computation.2 | async-start | bytes 4198400 | tf_op jit(solution)/shard_map/all_to_all | solution.py:15
  362.6 20.0 %copy-start.3 = (f32[256,256]{1,0:T(8,128)}, f32[256,256]{1,0:T(8,128)S(1)}, u32[]{:S(2)}) copy-start(f32[256,256]{1,0:T(8,128)S(1)} %fusion.50) | copy-start | bytes 786436
  382.6 34.2 %all-to-all-start.3 = ((f32[8,256,256]{1,2,0:T(8,128)}), f32[8,256,256]{1,2,0:T(8,128)}, u32[]{:S(2)}, u32[]{:S(2)}) async-start(f32[8,256,256]{1,2,0:T(8,128)} %broadcast_in_dim.20), calls=%async_computation.3 | async-start | bytes 4194304 | tf_op jit(solution)/shard_map/all_to_all | solution.py:22
  440.2 11.4 %copy-start.1 = (f32[1,2048,256]{2,1,0:T(8,128)S(1)}, f32[1,2048,256]{2,1,0:T(8,128)}, u32[]{:S(2)}) copy-start(f32[1,2048,256]{2,1,0:T(8,128)} %param.14) | copy-start | bytes 6291460
Sparse Core Ops, SparseCore 0:
  9.8 38.8 all-gather.16
  50.5 54.1 all-gather.18
  107.2 154.5 all-gather.8
  264.1 51.1 all-gather.10
  317.5 24.6 all-gather.12
  343.8 96.3 all-gather.14
